TPU v7x, 128 devices: a whole 4x4x4 slice. The times are simulated.
128 devices in a mesh: group: 8 (over x, core), dev: 16 (over y, z).
Axes of the slice: x: 4, y: 4, z: 4, core: 2. Of those that a mesh axis runs over, the one named last changes fastest.
Arguments:
- images: bfloat16 [16384, 1152], P(('group', 'dev')), may hold values from -1 to 1
- texts: bfloat16 [16384, 1152], P(('group', 'dev')), may hold values from -1 to 1
- lang_order: int32 [16384], P(('group', 'dev')), may hold values from 0 to 2047, as said below
- position: int32 [16384], P(('group', 'dev')), may hold values from 0 to 2047, as said below
- logit_scale: float32 [1], replicated, may hold values from 8 to 24
- logit_bias: float32 [1], replicated, may hold values from -4 to -1
Outputs:
- image_grad: float32 [16384, 1152], P(('group', 'dev'))
- text_grad: float32 [16384, 1152], P(('group', 'dev'))
- loss: float32 [1], replicated
Inputs may be any that keep to these rules, and one draw needn't show every extreme that they name: In each group of 2048 examples, lang_order is a permutation of the group-local indices; the 128 entries of one device name at most 16 examples held by any one device of the group, and exactly 16 for each device they name. position is the inverse of lang_order within each group.
All inputs are finite; a program needn't handle non-finite values.
Results may differ from a plain program's by a relative error of at most 0.00062.
Values may be sent and summed in bfloat16 or wider, within the bound.
A program may use at most 64 MiB of HBM per device.

v0:
```python
import jax
import jax.numpy as jnp
from jax import lax
from jax.sharding import Mesh
from jax.sharding import PartitionSpec as P

DEV = ("dev_0", "dev_1")
GROUP = ("group_0", "group_1")
GROUP_DEV = ("group_0", "group_1", "dev_0", "dev_1")
EPSILON = 1e-06


def normalize(values):
    wide = values.astype(jnp.float32)
    recip = lax.rsqrt(jnp.sum(wide * wide, axis=1, keepdims=True) + EPSILON)
    return (wide * recip, recip)


def project_back(unit, recip, grad):
    return recip * (grad - unit * jnp.sum(unit * grad, axis=1, keepdims=True))


def per_device(images, texts, lang_order, position, logit_scale, logit_bias):
    row_count, width_count = images.shape
    dev_count = lax.axis_size(DEV)
    group_count = lax.axis_size(GROUP)
    scale = logit_scale[0]
    bias = logit_bias[0]
    span = row_count * dev_count
    group_index = lax.axis_index(GROUP)
    img_unit, img_recip = normalize(images)
    txt_unit, txt_recip = normalize(texts)
    img_block = lax.all_gather(img_unit.astype(jnp.bfloat16), DEV, axis=0, tiled=True)
    txt_block = lax.all_gather(txt_unit.astype(jnp.bfloat16), GROUP, axis=0, tiled=True)
    txt_ids = lax.all_gather(group_index * span + lang_order, GROUP, axis=0, tiled=True)
    img_ids = group_index * span + jnp.arange(span, dtype=jnp.int32)
    logits = (
        scale
        * lax.dot_general(
            img_block, txt_block, (((1,), (1,)), ((), ())), preferred_element_type=jnp.float32
        )
        + bias
    )
    sign = jnp.where(img_ids[:, None] == txt_ids[None, :], jnp.float32(1.0), jnp.float32(-1.0))
    loss_part = jnp.sum(-jax.nn.log_sigmoid(sign * logits))
    coeff = (-sign * jax.nn.sigmoid(-sign * logits)).astype(jnp.bfloat16)
    dimg_part = jnp.dot(coeff, txt_block, preferred_element_type=jnp.float32)
    dtext_part = lax.dot_general(
        coeff, img_block, (((0,), (0,)), ((), ())), preferred_element_type=jnp.float32
    )
    dimg = scale * lax.psum_scatter(dimg_part, DEV, scatter_dimension=0, tiled=True)
    dtext = scale * lax.psum_scatter(dtext_part, GROUP, scatter_dimension=0, tiled=True)
    total = jnp.float32(span * group_count)
    loss = (lax.psum(loss_part, GROUP_DEV) / (total * total)).reshape(1)
    return (project_back(img_unit, img_recip, dimg), project_back(txt_unit, txt_recip, dtext), loss)


def solution(mesh):
    finer = Mesh(mesh.devices.reshape(4, 2, 4, 4), GROUP_DEV)
    return jax.shard_map(
        per_device,
        mesh=finer,
        in_specs=(P(GROUP_DEV, None), P(GROUP_DEV, None), P(GROUP_DEV), P(GROUP_DEV), P(), P()),
        out_specs=(P(GROUP_DEV, None), P(GROUP_DEV, None), P()),
        check_vma=False,
    )
```

profile of v0, /device:TPU:0, one launch (start us, length us, event | category | flops | bytes accessed | tf_op | source)
XLA Modules:
  0.0 262.9 jit_solution(11099517485220100941)
XLA Ops:
  7.2 0.0 all-gather.6.cloned.1.call-start
  7.2 1.1 fusion.22
  8.3 1.8 fusion.11
  10.1 0.0 all-gather.6.cloned.1.call-update
  10.1 0.0 all-gather.4.cloned.1.call-start
  10.2 1.1 fusion.18
  11.3 1.8 fusion.14
  13.1 0.0 all-gather.4.cloned.1.call-update
  13.1 0.0 reduce-scatter.5.cloned.1.call-start
  14.5 0.7 add_bitcast_fusion
  15.1 10.6 %all-gather = s32[8,1,128]{2,1,0:T(1,128)S(1)} all-gather(s32[1,1,128]{2,1,0:T(1,128)S(1)} %add_bitcast_fusion), channel_id=1, replica_groups=mesh['group_0'=4,'group_1'=2,'dev_0'=4,'dev_1'=4] {'group_0','group_1'}, dimensions={0}, use_global_device_ids=true | all-gather | bytes 4608 | tf_op jit(solution)/shard_map/all_gather | solution.py:35
  25.8 12.5 %all-gather.6.cloned.1.call-done = bf16[1024,1152]{1,0:T(8,128)(2,1)} async-done(((bf16[128,1152]{1,0:T(8,128)(2,1)}), bf16[1024,1152]{1,0:T(8,128)(2,1)}) %all-gather.6.cloned.1.call-update) | async-done | bytes 2359312 | tf_op jit(solution)/shard_map/all_gather | solution.py:34
  38.3 57.3 %all-gather.4.cloned.1.call-done = bf16[2048,1152]{1,0:T(8,128)(2,1)} async-done(((bf16[128,1152]{1,0:T(8,128)(2,1)}), bf16[2048,1152]{1,0:T(8,128)(2,1)}) %all-gather.4.cloned.1.call-update) | async-done | bytes 4718608 | tf_op jit(solution)/shard_map/all_gather | solution.py:33
  95.6 0.0 copy-start.2
  95.6 16.4 %fusion.7 = (f32[]{:T(128)}, bf16[2048,1024]{1,0:T(8,128)(2,1)S(1)}) fusion(f32[]{:T(128)} %bitcast.17, f32[]{:T(128)} %bitcast.14, s32[1024]{0:T(1024)S(1)} %bitcast.18, s32[2048]{0:T(1024)S(1)} %iota_add_fusion, bf16[2048,1152]{1,0:T(8,128)(2,1)} %all-gather.4.cloned.1.call-done, bf16[1024,1152]{1,0:T(8,128)(2,1)} %all-gather.6.cloned.1.call-done), kind=kOutput, calls=%fused_computation.10 | convolution fusion | flops 4873781248 | bytes 11284492 | tf_op jit(solution)/shard_map/dot_general | solution.py:39
  112.0 0.0 copy-start.4
  112.0 1.9 copy-done.4
  113.9 0.0 copy-done.2
  113.9 0.0 copy-start.3
  113.9 7.6 %fusion.24 = f32[1024,1152]{1,0:T(8,128)} fusion(bf16[2048,1024]{1,0:T(8,128)(2,1)S(1)} %get-tuple-element.4, bf16[2048,1152]{1,0:T(8,128)(2,1)S(1)} %copy-done.2), kind=kOutput, calls=%fused_computation.36 | convolution fusion | flops 4831838208 | bytes 13631488 | tf_op jit(solution)/shard_map/dot_general | solution.py:48
  121.5 0.0 reduce-scatter.5.cloned.1.call-update
  121.5 0.0 reduce-scatter.3.cloned.1.call-start
  121.6 0.0 copy-done.3
  121.6 9.6 %fusion.23 = f32[2048,1152]{1,0:T(8,128)} fusion(bf16[2048,1024]{1,0:T(8,128)(2,1)} %copy-done.4, bf16[1024,1152]{1,0:T(8,128)(2,1)S(1)} %copy-done.3), kind=kOutput, calls=%fused_computation.35 | convolution fusion | flops 4831838208 | bytes 15990784 | tf_op jit(solution)/shard_map/dot_general | solution.py:47
  131.1 0.0 copy-start
  131.1 0.0 copy-start.1
  131.2 0.0 reduce-scatter.3.cloned.1.call-update
  131.2 65.9 %psum.7 = f32[]{:T(128)} all-reduce(f32[]{:T(128)} %get-tuple-element.3), channel_id=1, replica_groups=mesh['group_0'=4,'group_1'=2,'dev_0'=4,'dev_1'=4] {'group_0','group_1','..., use_global_device_ids=true, to_apply=%region_7.8 | all-reduce | flops 1 | bytes 8 | tf_op jit(solution)/shard_map/psum | solution.py:54
  197.7 0.0 reduce-scatter.5.cloned.1.call-done
  197.7 0.0 copy-done
  197.8 1.3 fusion.19
  199.1 2.1 fusion.21
  201.2 50.7 %reduce-scatter.3.cloned.1.call-done = f32[128,1152]{1,0:T(8,128)} async-done(((f32[2048,1152]{1,0:T(8,128)}), f32[128,1152]{1,0:T(8,128)}) %reduce-scatter.3.cloned.1.call-update) | async-done | bytes 589840 | tf_op jit(solution)/shard_map/reduce_scatter | solution.py:51
  251.8 0.0 copy-done.1
  251.8 1.3 fusion.15
  253.1 2.1 fusion.17
  (3 shorter events, 0.0 us)
Async XLA Ops:
  7.2 31.2 %all-gather.6.cloned.1.call-start = ((), (), s32[]{:S(2)}) async-start(), calls=%async_computation.3 | async-start | bytes 2654208 | tf_op jit(solution)/shard_map/all_gather | solution.py:34
  10.1 85.5 %all-gather.4.cloned.1.call-start = ((), (), s32[]{:S(2)}) async-start(), calls=%async_computation.2 | async-start | bytes 5013504 | tf_op jit(solution)/shard_map/all_gather | solution.py:33
  13.1 184.6 %reduce-scatter.5.cloned.1.call-start = ((), (), s32[]{:S(2)}) async-start(), calls=%async_computation.5 | async-start | bytes 5308416 | tf_op jit(solution)/shard_map/reduce_scatter | solution.py:52
  95.6 18.3 %copy-start.2 = (bf16[2048,1152]{1,0:T(8,128)(2,1)S(1)}, bf16[2048,1152]{1,0:T(8,128)(2,1)}, u32[]{:S(2)}) copy-start(bf16[2048,1152]{1,0:T(8,128)(2,1)} %all-gather.4.cloned.1.call-done) | copy-start | bytes 14155780
  112.0 1.9 copy-start.4
  113.9 7.6 %copy-start.3 = (bf16[1024,1152]{1,0:T(8,128)(2,1)S(1)}, bf16[1024,1152]{1,0:T(8,128)(2,1)}, u32[]{:S(2)}) copy-start(bf16[1024,1152]{1,0:T(8,128)(2,1)} %all-gather.6.cloned.1.call-done) | copy-start | bytes 7077892
  121.5 130.3 %reduce-scatter.3.cloned.1.call-start = ((), (), s32[]{:S(2)}) async-start(), calls=%async_computation.4 | async-start | bytes 10027008 | tf_op jit(solution)/shard_map/reduce_scatter | solution.py:51
  131.1 66.6 %copy-start = (bf16[128,1152]{1,0:T(8,128)(2,1)S(1)}, bf16[128,1152]{1,0:T(8,128)(2,1)}, u32[]{:S(2)}) copy-start(bf16[128,1152]{1,0:T(8,128)(2,1)} %param.7) | copy-start | bytes 884740
  131.1 120.7 %copy-start.1 = (bf16[128,1152]{1,0:T(8,128)(2,1)S(1)}, bf16[128,1152]{1,0:T(8,128)(2,1)}, u32[]{:S(2)}) copy-start(bf16[128,1152]{1,0:T(8,128)(2,1)} %param.6) | copy-start | bytes 884740
Sparse Core Ops, SparseCore 0:
  10.3 28.0 all-gather.5
  41.1 54.4 all-gather.3
  121.6 39.0 reduce-scatter.4
  164.1 87.6 reduce-scatter.2
where the time goes:
time: 263 us
  waiting for transfers between devices  121 us (46%)
  blocking collectives  76.5 us (29%)
  matrix products  33.5 us (13%)
  between operations  16.9 us (6%)
  other arithmetic  13.3 us (5%)
    psum x1, blocking collectives, per_device(): loss = (lax.psum(loss_part, GROUP_DEV) / (total * total)).reshape(1)  65.9 us
    all_gather x1, waiting for transfers between devices, per_device(): lax.all_gather(img_unit.astype(jnp.bfloat16), DEV, axis=0, tiled=True)  57.3 us
    reduce_scatter x1, waiting for transfers between devices, per_device(): lax.psum_scatter(dimg_part, DEV, scatter_dimension=0, tiled=True)  50.7 us
    dot_general x1, matrix products, per_device(): lax.dot_general(img_block, txt_block, (((1,), (1,)), ((), ())), preferred...  16.4 us
    all_gather x1, waiting for transfers between devices, per_device(): lax.all_gather(txt_unit.astype(jnp.bfloat16), GROUP, axis=0, tiled=True)  12.5 us
    all_gather x1, blocking collectives, per_device(): lax.all_gather(group_index * span + lang_order, GROUP, axis=0, tiled=True)  10.6 us
    dot_general x1, matrix products, per_device(): dimg_part = jnp.dot(coeff, txt_block, preferred_element_type=jnp.float32)  9.57 us
    dot_general x1, matrix products, per_device(): lax.dot_general(coeff, img_block, (((0,), (0,)), ((), ())), preferred_ele...  7.55 us
  transfers between devices with their start and end apart: 4, of which 3 were waited for; matrix products, arithmetic and copies ran while one was open for 6% of the time, Pallas kernels for 0%

commit v1 on v0

--- a/solution.py
+++ b/solution.py
@@ -8,6 +8,9 @@
 GROUP = ("group_0", "group_1")
 GROUP_DEV = ("group_0", "group_1", "dev_0", "dev_1")
 EPSILON = 1e-06
+wall_attach = lambda own_rows: jnp.concatenate(
+    lax.all_to_all(jnp.stack([own_rows] * lax.axis_size(DEV)), DEV, 0, 0), 0
+)
 
 
 def normalize(values):
@@ -30,7 +33,7 @@
     group_index = lax.axis_index(GROUP)
     img_unit, img_recip = normalize(images)
     txt_unit, txt_recip = normalize(texts)
-    img_block = lax.all_gather(img_unit.astype(jnp.bfloat16), DEV, axis=0, tiled=True)
+    img_block = wall_attach(img_unit.astype(jnp.bfloat16))
     txt_block = lax.all_gather(txt_unit.astype(jnp.bfloat16), GROUP, axis=0, tiled=True)
     txt_ids = lax.all_gather(group_index * span + lang_order, GROUP, axis=0, tiled=True)
     img_ids = group_index * span + jnp.arange(span, dtype=jnp.int32)

time: 263 us -> 268 us (1.019)
  waiting for transfers between devices: 121 us -> 110 us
  starting transfers between devices: 0.16 us -> 8.51 us
  blocking collectives: 76.5 us -> 81.3 us
  other arithmetic: 13.3 us -> 10 us
  local copies, waits for them, and re-layouts: 1.96 us -> 4.76 us
    all_gather x1 -> x0, waiting for transfers between devices: 57.3 us -> none  [per_device(): lax.all_gather(img_unit.astype(jnp.bfloat16), DEV, axis=0, tiled=True)]
    all_to_all x0 -> x1, waiting for transfers between devices: none -> 41.7 us  [lax.all_to_all(jnp.stack([own_rows] * lax.axis_size(DEV)), DEV, 0, 0)]
    all_to_all x0 -> x1, starting transfers between devices: none -> 8.2 us  [lax.all_to_all(jnp.stack([own_rows] * lax.axis_size(DEV)), DEV, 0, 0)]
    psum x1, blocking collectives: 65.9 us -> 70.7 us  [per_device(): loss = (lax.psum(loss_part, GROUP_DEV) / (total * total)).reshape(1)]
    all_gather x1, waiting for transfers between devices: 12.5 us -> 17.1 us  [per_device(): lax.all_gather(txt_unit.astype(jnp.bfloat16), GROUP, axis=0, tiled=True)]
    another operation x0 -> x1, local copies, waits for them, and re-layouts: none -> 2.8 us  [jnp.stack([own_rows] * lax.axis_size(DEV))]
  transfers between devices with their start and end apart: 4 -> 4, of which waited for: 3 -> 3; matrix products, arithmetic and copies ran while one was open for 6% -> 5% of each run, Pallas kernels for 0% -> 0%
where the time goes in v1:
time: 268 us
  waiting for transfers between devices  110 us (41%)
  blocking collectives  81.3 us (30%)
  matrix products  35.8 us (13%)
  between operations  16.9 us (6%)
  other arithmetic  10 us (4%)
  starting transfers between devices  8.51 us (3%)
  local copies, waits for them, and re-layouts  4.76 us (2%)
    psum x1, blocking collectives, per_device(): loss = (lax.psum(loss_part, GROUP_DEV) / (total * total)).reshape(1)  70.7 us
    reduce_scatter x1, waiting for transfers between devices, per_device(): lax.psum_scatter(dimg_part, DEV, scatter_dimension=0, tiled=True)  51.5 us
    all_to_all x1, waiting for transfers between devices, lax.all_to_all(jnp.stack([own_rows] * lax.axis_size(DEV)), DEV, 0, 0)  41.7 us
    all_gather x1, waiting for transfers between devices, per_device(): lax.all_gather(txt_unit.astype(jnp.bfloat16), GROUP, axis=0, tiled=True)  17.1 us
    dot_general x1, matrix products, per_device(): lax.dot_general(img_block, txt_block, (((1,), (1,)), ((), ())), preferred...  16.2 us
    all_gather x1, blocking collectives, per_device(): lax.all_gather(group_index * span + lang_order, GROUP, axis=0, tiled=True)  10.6 us
    dot_general x1, matrix products, per_device(): lax.dot_general(coeff, img_block, (((0,), (0,)), ((), ())), preferred_ele...  10 us
    dot_general x1, matrix products, per_device(): dimg_part = jnp.dot(coeff, txt_block, preferred_element_type=jnp.float32)  9.57 us
  transfers between devices with their start and end apart: 4, of which 3 were waited for; matrix products, arithmetic and copies ran while one was open for 5% of the time, Pallas kernels for 0%

profile of v1, /device:TPU:0, one launch (start us, length us, event | category | flops | bytes accessed | tf_op | source)
XLA Modules:
  0.0 267.7 jit_solution(12037374779891629184)
XLA Ops:
  7.2 0.0 copy-start
  7.2 0.0 copy-start.3
  7.2 1.1 fusion.18
  8.3 1.1 fusion.14
  9.4 2.8 %stack.2 = bf16[16,128,1152]{2,1,0:T(8,128)(2,1)} broadcast(bf16[128,1152]{1,0:T(8,128)(2,1)S(1)} %fusion.14), dimensions={1,2} | broadcast | bytes 5013504 | tf_op jit(solution)/shard_map/stack | solution.py:12
  12.2 8.2 %all-to-all-start = ((bf16[16,128,1152]{2,1,0:T(8,128)(2,1)}), bf16[16,128,1152]{2,1,0:T(8,128)(2,1)}, u32[]{:S(2)}, u32[]{:S(2)}) async-start(bf16[16,128,1152]{2,1,0:T(8,128)(2,1)} %stack.2), calls=%async_computation | async-start | bytes 9437184 | tf_op jit(solution)/shard_map/all_to_all | solution.py:12
  20.4 0.0 all-gather.3.cloned.1.call-start
  20.5 0.0 copy-done
  20.5 0.1 fusion.22
  20.6 0.8 fusion.11
  21.5 0.0 all-gather.3.cloned.1.call-update
  21.5 0.0 reduce-scatter.5.cloned.1.call-start
  22.9 0.0 copy-done.3
  22.9 10.6 %all-gather = s32[8,1,128]{2,1,0:T(1,128)S(1)} all-gather(s32[1,1,128]{2,1,0:T(1,128)S(1)} %add_bitcast_fusion), channel_id=1, replica_groups=mesh['group_0'=4,'group_1'=2,'dev_0'=4,'dev_1'=4] {'group_0','group_1'}, dimensions={0}, use_global_device_ids=true | all-gather | bytes 4608 | tf_op jit(solution)/shard_map/all_gather | solution.py:38
  33.4 17.1 %all-gather.3.cloned.1.call-done = bf16[1024,1152]{1,0:T(8,128)(2,1)} async-done(((bf16[128,1152]{1,0:T(8,128)(2,1)}), bf16[1024,1152]{1,0:T(8,128)(2,1)}) %all-gather.3.cloned.1.call-update) | async-done | bytes 2359312 | tf_op jit(solution)/shard_map/all_gather | solution.py:37
  50.6 41.7 %all-to-all-done = bf16[16,128,1152]{2,1,0:T(8,128)(2,1)} async-done(((bf16[16,128,1152]{2,1,0:T(8,128)(2,1)}), bf16[16,128,1152]{2,1,0:T(8,128)(2,1)}, u32[]{:S(2)}, u32[]{:S(2)}) %all-to-all-start) | async-done | bytes 4718624 | tf_op jit(solution)/shard_map/all_to_all | solution.py:12
  92.3 16.2 %fusion.7 = (f32[]{:T(128)}, bf16[2048,1024]{1,0:T(8,128)(2,1)S(1)}) fusion(f32[]{:T(128)} %bitcast.18, f32[]{:T(128)} %bitcast.15, s32[1024]{0:T(1024)S(1)} %bitcast.19, s32[2048]{0:T(1024)S(1)} %iota_add_fusion, bf16[2048,1152]{1,0:T(8,128)(2,1)} %bitcast.3, bf16[1024,1152]{1,0:T(8,128)(2,1)} %all-gather.3.cloned.1.call-done), kind=kOutput, calls=%fused_computation.10 | convolution fusion | flops 4873781248 | bytes 11284492 | tf_op jit(solution)/shard_map/dot_general | solution.py:42
  108.5 0.0 copy-start.4
  108.5 1.9 copy-done.4
  110.5 0.0 copy-start.2
  110.5 10.0 %fusion.24 = f32[1024,1152]{1,0:T(8,128)} fusion(bf16[2048,1024]{1,0:T(8,128)(2,1)S(1)} %get-tuple-element.4, bf16[2048,1152]{1,0:T(8,128)(2,1)} %bitcast.3), kind=kOutput, calls=%fused_computation.36 | convolution fusion | flops 4831838208 | bytes 13631488 | tf_op jit(solution)/shard_map/dot_general | solution.py:51
  120.5 0.0 reduce-scatter.5.cloned.1.call-update
  120.5 0.2 reduce-scatter.3.cloned.1.call-start
  120.7 0.0 copy-done.2
  120.7 9.6 %fusion.23 = f32[2048,1152]{1,0:T(8,128)} fusion(bf16[2048,1024]{1,0:T(8,128)(2,1)} %copy-done.4, bf16[1024,1152]{1,0:T(8,128)(2,1)S(1)} %copy-done.2), kind=kOutput, calls=%fused_computation.35 | convolution fusion | flops 4831838208 | bytes 15990784 | tf_op jit(solution)/shard_map/dot_general | solution.py:50
  130.3 0.0 copy-start.1
  130.3 0.0 reduce-scatter.3.cloned.1.call-update
  130.3 70.7 %psum.7 = f32[]{:T(128)} all-reduce(f32[]{:T(128)} %get-tuple-element.3), channel_id=1, replica_groups=mesh['group_0'=4,'group_1'=2,'dev_0'=4,'dev_1'=4] {'group_0','group_1','..., use_global_device_ids=true, to_apply=%region_7.8 | all-reduce | flops 1 | bytes 8 | tf_op jit(solution)/shard_map/psum | solution.py:57
  201.7 0.0 reduce-scatter.5.cloned.1.call-done
  201.7 1.3 fusion.19
  203.0 2.1 fusion.21
  205.1 51.5 %reduce-scatter.3.cloned.1.call-done = f32[128,1152]{1,0:T(8,128)} async-done(((f32[2048,1152]{1,0:T(8,128)}), f32[128,1152]{1,0:T(8,128)}) %reduce-scatter.3.cloned.1.call-update) | async-done | bytes 589840 | tf_op jit(solution)/shard_map/reduce_scatter | solution.py:54
  256.6 0.0 copy-done.1
  256.6 1.3 fusion.15
  257.9 2.1 fusion.17
  (4 shorter events, 0.0 us)
Async XLA Ops:
  7.2 13.3 %copy-start = (bf16[128,1152]{1,0:T(8,128)(2,1)S(1)}, bf16[128,1152]{1,0:T(8,128)(2,1)}, u32[]{:S(2)}) copy-start(bf16[128,1152]{1,0:T(8,128)(2,1)} %param.7) | copy-start | bytes 884740
  7.2 15.7 %copy-start.3 = (s32[128]{0:T(128)S(1)}, s32[128]{0:T(128)}, u32[]{:S(2)}) copy-start(s32[128]{0:T(128)} %param.8) | copy-start | bytes 1540
  12.2 80.1 %all-to-all-start = ((bf16[16,128,1152]{2,1,0:T(8,128)(2,1)}), bf16[16,128,1152]{2,1,0:T(8,128)(2,1)}, u32[]{:S(2)}, u32[]{:S(2)}) async-start(bf16[16,128,1152]{2,1,0:T(8,128)(2,1)} %stack.2), calls=%async_computation | async-start | bytes 9437184 | tf_op jit(solution)/shard_map/all_to_all | solution.py:12
  20.4 30.2 %all-gather.3.cloned.1.call-start = ((), (), s32[]{:S(2)}) async-start(), calls=%async_computation.3 | async-start | bytes 2654208 | tf_op jit(solution)/shard_map/all_gather | solution.py:37
  21.5 180.2 %reduce-scatter.5.cloned.1.call-start = ((), (), s32[]{:S(2)}) async-start(), calls=%async_computation.5 | async-start | bytes 5308416 | tf_op jit(solution)/shard_map/reduce_scatter | solution.py:55
  108.5 1.9 copy-start.4
  110.5 10.3 %copy-start.2 = (bf16[1024,1152]{1,0:T(8,128)(2,1)S(1)}, bf16[1024,1152]{1,0:T(8,128)(2,1)}, u32[]{:S(2)}) copy-start(bf16[1024,1152]{1,0:T(8,128)(2,1)} %all-gather.3.cloned.1.call-done) | copy-start | bytes 7077892
  120.5 136.1 %reduce-scatter.3.cloned.1.call-start = ((), (), s32[]{:S(2)}) async-start(), calls=%async_computation.4 | async-start | bytes 10027008 | tf_op jit(solution)/shard_map/reduce_scatter | solution.py:54
  130.3 126.3 %copy-start.1 = (bf16[128,1152]{1,0:T(8,128)(2,1)S(1)}, bf16[128,1152]{1,0:T(8,128)(2,1)}, u32[]{:S(2)}) copy-start(bf16[128,1152]{1,0:T(8,128)(2,1)} %param.6) | copy-start | bytes 884740
Sparse Core Ops, SparseCore 0:
  23.5 27.0 all-gather.2
  120.6 44.6 reduce-scatter.4
  168.8 87.7 reduce-scatter.2
